TPU v7x, 256 devices: a whole 4x4x8 slice. The times are simulated.
256 devices in a mesh: kx: 16 (over y_lo, x, core), ky: 16 (over y_hi, z).
Axes of the slice: x: 4, y: 4 (y_hi: 2, y_lo: 2; y = y_hi * 2 + y_lo), z: 8, core: 2. Of those that a mesh axis runs over, the one named last changes fastest.
Arguments:
- coeffs: bfloat16 [16, 16, 2, 36, 128, 256], P('kx', 'ky'), may hold values from -1 to 1, as said below
- bands: int32 [32], replicated, may hold values from 0 to 35, as said below
- umklapp: int32 [2, 2], replicated, may hold values from -3 to 3
Outputs:
- flux: float32 [16, 16, 2], P('kx', 'ky')
- links: float32 [16, 16, 3, 2], P('kx', 'ky')
Inputs may be any that keep to these rules, and one draw needn't show every extreme that they name: 32 different indices of stored bands. `coeffs`: coefficients of order 1 / sqrt(32768); link matrices between neighbouring k-points stay close enough to unitary that elimination without row exchanges has pivots of magnitude near one.
All inputs are finite; a program needn't handle non-finite values.
Results may differ from a plain program's by a relative error of at most 0.0003.
Values may be sent and summed in bfloat16 or wider, within the bound.
A program may use at most 128 MiB of HBM per device.

v0:
```python
import jax
import jax.numpy as jnp
from jax import lax
from jax.sharding import PartitionSpec as P


def passed_along(block, axis, distance):
    devices = range(lax.axis_size(axis))
    route = [((i - distance) % len(devices), i) for i in devices]
    return lax.ppermute(block, axis, route)


def correlation(left_block, right_block):
    count = left_block.shape[1]
    left_rows = left_block.reshape(2 * count, -1)
    right_rows = right_block.reshape(2 * count, -1)
    square = lax.dot_general(
        left_rows, right_rows, (((1,), (1,)), ((), ())), preferred_element_type=jnp.float32
    )
    real_part = square[:count, :count] + square[count:, count:]
    imag_part = square[:count, count:] - square[count:, :count]
    return (real_part, imag_part)


def det_units(real_stack, imag_stack):
    count = real_stack.shape[1]
    places = jnp.arange(count, dtype=jnp.int32)

    def elimination(pivot_row, carry):
        work_real, work_imag, unit_real, unit_imag = carry
        pivot_real = work_real[:, pivot_row, pivot_row]
        pivot_imag = work_imag[:, pivot_row, pivot_row]
        square_mag = pivot_real * pivot_real + pivot_imag * pivot_imag
        inverse_real = pivot_real / square_mag
        inverse_imag = -pivot_imag / square_mag
        column_real = work_real[:, :, pivot_row]
        column_imag = work_imag[:, :, pivot_row]
        below = (places > pivot_row).astype(jnp.float32)[None, :]
        factor_real = (
            column_real * inverse_real[:, None] - column_imag * inverse_imag[:, None]
        ) * below
        factor_imag = (
            column_real * inverse_imag[:, None] + column_imag * inverse_real[:, None]
        ) * below
        row_real = work_real[:, pivot_row, :]
        row_imag = work_imag[:, pivot_row, :]
        work_real = work_real - (
            factor_real[:, :, None] * row_real[:, None, :]
            - factor_imag[:, :, None] * row_imag[:, None, :]
        )
        work_imag = work_imag - (
            factor_real[:, :, None] * row_imag[:, None, :]
            + factor_imag[:, :, None] * row_real[:, None, :]
        )
        magnitude = jnp.sqrt(square_mag)
        next_real = (unit_real * pivot_real - unit_imag * pivot_imag) / magnitude
        next_imag = (unit_real * pivot_imag + unit_imag * pivot_real) / magnitude
        return (work_real, work_imag, next_real, next_imag)

    batch = real_stack.shape[0]
    start = (
        real_stack,
        imag_stack,
        jnp.ones((batch,), jnp.float32),
        jnp.zeros((batch,), jnp.float32),
    )
    result = lax.fori_loop(0, count, elimination, start)
    return jnp.stack([result[2], result[3]], axis=-1)


def rolled(block, offset):
    return jnp.roll(block, (offset[0], offset[1]), axis=(2, 3))


def times(first, second):
    return jnp.stack(
        [
            first[..., 0] * second[..., 0] - first[..., 1] * second[..., 1],
            first[..., 0] * second[..., 1] + first[..., 1] * second[..., 0],
        ],
        axis=-1,
    )


def conjugate(value):
    return jnp.stack([value[..., 0], -value[..., 1]], axis=-1)


def per_device(coeffs, bands, umklapp):
    own_block = jnp.take(coeffs[0, 0], bands, axis=1)
    zero_shift = jnp.zeros((2,), jnp.int32)
    ky_count = lax.axis_size("ky")
    at_ky_edge = lax.axis_index("ky") == ky_count - 1
    shift_x = jnp.where(lax.axis_index("kx") == lax.axis_size("kx") - 1, umklapp[0], zero_shift)
    shift_y = jnp.where(at_ky_edge, umklapp[1], zero_shift)
    right_block = passed_along(own_block, "kx", -1)
    upper_block = passed_along(own_block, "ky", -1)
    corner_block = passed_along(upper_block, "kx", -1)
    pairs = [
        correlation(own_block, rolled(right_block, shift_x)),
        correlation(own_block, rolled(upper_block, shift_y)),
        correlation(own_block, rolled(corner_block, shift_x + shift_y)),
    ]
    units = det_units(jnp.stack([p[0] for p in pairs]), jnp.stack([p[1] for p in pairs]))
    along_x, along_y, along_d = (units[0], units[1], units[2])
    y_next = passed_along(along_y, "kx", -1)
    x_next = passed_along(along_x, "ky", -1)
    first = times(times(along_x, y_next), conjugate(along_d))
    second = times(times(along_d, conjugate(x_next)), conjugate(along_y))
    flux = jnp.stack([jnp.arctan2(first[1], first[0]), jnp.arctan2(second[1], second[0])])
    links = jnp.stack([along_x, along_y, along_d])
    return (flux.reshape(1, 1, 2), links.reshape(1, 1, 3, 2))


def solution(mesh):
    in_specs = (P("kx", "ky", None, None, None, None), P(), P())
    out_specs = (P("kx", "ky", None), P("kx", "ky", None, None))
    return jax.shard_map(
        per_device, mesh=mesh, in_specs=in_specs, out_specs=out_specs, check_vma=False
    )
```

profile of v0, /device:TPU:1, one launch (start us, length us, event | category | flops | bytes accessed | tf_op | source)
XLA Modules:
  0.0 264.6 jit_solution(3685167412318647988)
XLA Ops:
  2.0 5.1 %gather_fusion = bf16[32,2,128,256]{3,2,1,0:T(8,128)(2,1)} fusion(bf16[2,36,128,256]{3,2,1,0:T(8,128)(2,1)} %bitcast.81, s32[1024]{0:T(1024)S(1)} %pad_clamp_fusion), kind=kCustom, calls=%fused_computation | custom fusion | bytes 8388736 | tf_op jit(solution)/shard_map/jit(_take)/gather | solution.py:90
  7.1 4.7 %select_bitcast_fusion = bf16[2,32,128,256]{3,2,0,1:T(8,128)(2,1)} fusion(bf16[32,2,128,256]{3,2,1,0:T(8,128)(2,1)} %gather_fusion, pred[32]{0:T(512)(128)(4,1)S(1)} %compare_and_fusion), kind=kLoop, calls=%fused_computation.40 | loop fusion | flops 2097152 | bytes 8388640 | tf_op jit(solution)/shard_map/jit(_take)/select_n | solution.py:90
  11.7 9.0 %collective-permute-start.1 = (bf16[2,32,128,256]{3,2,0,1:T(8,128)(2,1)}, bf16[2,32,128,256]{3,2,0,1:T(8,128)(2,1)}, u32[]{:S(2)}, u32[]{:S(2)}) collective-permute-start(bf16[2,32,128,256]{3,2,0,1:T(8,128)(2,1)} %select_bitcast_fusion), channel_id=1, source_target_pairs={{1,0},{2,1},{3,2},{4,3},{5,4},{6,5},{7,6},{8,7},{9,8},{10,9},{11,1... | collective-permute-start | bytes 12582920 | tf_op jit(solution)/shard_map/ppermute | solution.py:10
  20.8 1.0 collective-permute-start
  21.7 88.6 %collective-permute-done.1 = bf16[2,32,128,256]{3,2,0,1:T(8,128)(2,1)} collective-permute-done((bf16[2,32,128,256]{3,2,0,1:T(8,128)(2,1)}, bf16[2,32,128,256]{3,2,0,1:T(8,128)(2,1)}, u32[]{:S(2)}, u32[]{:S(2)}) %collective-permute-start.1) | collective-permute-done | bytes 4194336 | tf_op jit(solution)/shard_map/ppermute | solution.py:10
  110.3 1.5 collective-permute-start.2
  111.9 0.7 fusion.25
  116.5 4.6 %copy.27 = bf16[2,32,128,256]{3,2,1,0:T(8,128)(2,1)} copy(bf16[2,32,128,256]{3,2,0,1:T(8,128)(2,1)} %select_bitcast_fusion) | data formatting | bytes 8388608 | tf_op jit(solution)/shard_map/jit(_take)/select_n | solution.py:90
  129.3 6.7 %copy.35 = bf16[8,8,128,256]{3,1,2,0:T(8,128)(2,1)} copy(bf16[8,8,128,256]{3,2,1,0:T(8,128)(2,1)} %bitcast.74) | data formatting | bytes 8388608
  136.0 4.8 %fusion.8 = bf16[2,32,128,256]{3,2,0,1:T(8,128)(2,1)S(1)} fusion(s32[]{:T(128)S(6)} %select_n.95, bf16[2,32,128,256]{3,2,0,1:T(8,128)(2,1)} %collective-permute-done), kind=kLoop, calls=%fused_computation.39 | loop fusion | flops 8388608 | bytes 8388612 | tf_op jit(solution)/shard_map/jit(_roll_dynamic)/concatenate | solution.py:72
  140.9 3.5 %fusion.7 = bf16[2,32,128,256]{3,2,0,1:T(8,128)(2,1)S(1)} fusion(s32[]{:T(128)S(6)} %select_n.97, bf16[2,32,128,256]{3,2,0,1:T(8,128)(2,1)S(1)} %fusion.8), kind=kLoop, calls=%fused_computation.38 | loop fusion | flops 8388608 | bytes 8388612 | tf_op jit(solution)/shard_map/jit(_roll_dynamic)/concatenate | solution.py:72
  144.9 2.6 copy.36
  147.5 4.8 %fusion.6 = bf16[2,32,128,256]{3,2,0,1:T(8,128)(2,1)S(1)} fusion(s32[]{:T(128)S(6)} %select_n.99, bf16[2,32,128,256]{3,2,0,1:T(8,128)(2,1)} %collective-permute-done.1), kind=kLoop, calls=%fused_computation.37 | loop fusion | flops 8388608 | bytes 8388612 | tf_op jit(solution)/shard_map/jit(_roll_dynamic)/concatenate | solution.py:72
  152.4 3.8 %fusion.5 = bf16[2,32,128,256]{3,2,0,1:T(8,128)(2,1)S(1)} fusion(s32[]{:T(128)S(6)} %select_n.101, bf16[2,32,128,256]{3,2,0,1:T(8,128)(2,1)S(1)} %fusion.6), kind=kLoop, calls=%fused_computation.36 | loop fusion | flops 8388608 | bytes 8388612 | tf_op jit(solution)/shard_map/jit(_roll_dynamic)/concatenate | solution.py:72
  156.7 2.6 copy.37
  159.3 1.2 fusion.28
  160.6 1.2 fusion.29
  161.9 4.8 %fusion.4 = bf16[2,32,128,256]{3,2,0,1:T(8,128)(2,1)S(1)} fusion(s32[]{:T(128)S(6)} %select_n.103, bf16[2,32,128,256]{3,2,0,1:T(8,128)(2,1)} %collective-permute-done.2), kind=kLoop, calls=%fused_computation.35 | loop fusion | flops 8388608 | bytes 8388612 | tf_op jit(solution)/shard_map/jit(_roll_dynamic)/concatenate | solution.py:72
  166.8 3.8 %fusion.3 = bf16[2,32,128,256]{3,2,0,1:T(8,128)(2,1)S(1)} fusion(s32[]{:T(128)S(6)} %select_n.105, bf16[2,32,128,256]{3,2,0,1:T(8,128)(2,1)S(1)} %fusion.4), kind=kLoop, calls=%fused_computation.34 | loop fusion | flops 8388608 | bytes 8388612 | tf_op jit(solution)/shard_map/jit(_roll_dynamic)/concatenate | solution.py:72
  171.1 2.6 copy.38
  173.7 1.2 fusion.30
  175.2 19.8 %while.20 = (s32[]{:T(128)}, f32[3,32,32]{1,2,0:T(8,128)S(1)}, f32[3,32,32]{1,2,0:T(8,128)S(1)}, f32[3]{0:T(128)S(1)}, f32[3]{0:T(128)S(1)}, /*index=5*/s32[]{:T(128)}, s32[]{:T(128)}) while((s32[]{:T(128)}, f32[3,32,32]{1,2,0:T(8,128)S(1)}, f32[3,32,32]{1,2,0:T(8,128)S(1)}, f32[3]{0:T(128)S(1)}, f32[3]{0:T(128)S(1)}, ...), condition=%wide.region_1.3_spmd.clone, body=%wide.region_0.0_spmd.clone.sunk | while | flops 25459 | bytes 55823 | solution.py:67
  197.0 45.9 %collective-permute-start.3 = (f32[2]{0:T(128)S(1)}, f32[2]{0:T(128)S(1)}, u32[]{:S(2)}, u32[]{:S(2)}) collective-permute-start(f32[2]{0:T(128)S(1)} %get-tuple-element.155), channel_id=1, source_target_pairs={{16,0},{32,16},{48,32},{64,48},{80,64},{96,80},{112,96},{128,112},... | collective-permute-start | bytes 32 | tf_op jit(solution)/shard_map/ppermute | solution.py:10
  243.5 6.8 %collective-permute-start.4 = (f32[2]{0:T(128)S(1)}, f32[2]{0:T(128)S(1)}, u32[]{:S(2)}, u32[]{:S(2)}) collective-permute-start(f32[2]{0:T(128)S(1)} %get-tuple-element.156), channel_id=1, source_target_pairs={{1,0},{2,1},{3,2},{4,3},{5,4},{6,5},{7,6},{8,7},{9,8},{10,9},{11,1... | collective-permute-start | bytes 32 | tf_op jit(solution)/shard_map/ppermute | solution.py:10
  (288 shorter events, 26.2 us)
Async XLA Ops:
  7.1 104.8 %copy-start.1 = (s32[2,2]{1,0:T(2,128)S(1)}, s32[2,2]{1,0:T(2,128)}, u32[]{:S(2)}) copy-start(s32[2,2]{1,0:T(2,128)} %param.9) | copy-start | bytes 52
  11.7 98.6 %collective-permute-start.1 = (bf16[2,32,128,256]{3,2,0,1:T(8,128)(2,1)}, bf16[2,32,128,256]{3,2,0,1:T(8,128)(2,1)}, u32[]{:S(2)}, u32[]{:S(2)}) collective-permute-start(bf16[2,32,128,256]{3,2,0,1:T(8,128)(2,1)} %select_bitcast_fusion), channel_id=1, source_target_pairs={{1,0},{2,1},{3,2},{4,3},{5,4},{6,5},{7,6},{8,7},{9,8},{10,9},{11,1... | collective-permute-start | bytes 12582920 | tf_op jit(solution)/shard_map/ppermute | solution.py:10
  20.8 115.3 %collective-permute-start = (bf16[2,32,128,256]{3,2,0,1:T(8,128)(2,1)}, bf16[2,32,128,256]{3,2,0,1:T(8,128)(2,1)}, u32[]{:S(2)}, u32[]{:S(2)}) collective-permute-start(bf16[2,32,128,256]{3,2,0,1:T(8,128)(2,1)} %select_bitcast_fusion), channel_id=1, source_target_pairs={{16,0},{32,16},{48,32},{64,48},{80,64},{96,80},{112,96},{128,112},... | collective-permute-start | bytes 12582920 | tf_op jit(solution)/shard_map/ppermute | solution.py:10
  110.3 51.6 %collective-permute-start.2 = (bf16[2,32,128,256]{3,2,0,1:T(8,128)(2,1)}, bf16[2,32,128,256]{3,2,0,1:T(8,128)(2,1)}, u32[]{:S(2)}, u32[]{:S(2)}) collective-permute-start(bf16[2,32,128,256]{3,2,0,1:T(8,128)(2,1)} %collective-permute-done.1), channel_id=1, source_target_pairs={{16,0},{32,16},{48,32},{64,48},{80,64},{96,80},{112,96},{128,112},... | collective-permute-start | bytes 12582920 | tf_op jit(solution)/shard_map/ppermute | solution.py:10
  156.7 2.6 copy-start
  197.0 53.9 %collective-permute-start.3 = (f32[2]{0:T(128)S(1)}, f32[2]{0:T(128)S(1)}, u32[]{:S(2)}, u32[]{:S(2)}) collective-permute-start(f32[2]{0:T(128)S(1)} %get-tuple-element.155), channel_id=1, source_target_pairs={{16,0},{32,16},{48,32},{64,48},{80,64},{96,80},{112,96},{128,112},... | collective-permute-start | bytes 32 | tf_op jit(solution)/shard_map/ppermute | solution.py:10
  243.5 14.2 %collective-permute-start.4 = (f32[2]{0:T(128)S(1)}, f32[2]{0:T(128)S(1)}, u32[]{:S(2)}, u32[]{:S(2)}) collective-permute-start(f32[2]{0:T(128)S(1)} %get-tuple-element.156), channel_id=1, source_target_pairs={{1,0},{2,1},{3,2},{4,3},{5,4},{6,5},{7,6},{8,7},{9,8},{10,9},{11,1... | collective-permute-start | bytes 32 | tf_op jit(solution)/shard_map/ppermute | solution.py:10
where the time goes:
time: 265 us
  waiting for transfers between devices  88.6 us (33%)
  starting transfers between devices  64.2 us (24%)
  local copies, waits for them, and re-layouts  41.5 us (16%)
  other arithmetic  39.9 us (15%)
  between operations  25.6 us (10%)
  matrix products  3.68 us (1%)
    ppermute x5, waiting for transfers between devices, passed_along(): return lax.ppermute(block, axis, route)  88.6 us
    ppermute x5, starting transfers between devices, passed_along(): return lax.ppermute(block, axis, route)  64.2 us
    concatenate x6, other arithmetic, rolled(): return jnp.roll(block, (offset[0], offset[1]), axis=(2, 3))  25.6 us
    unnamed x10, local copies, waits for them, and re-layouts  14.7 us
    dynamic_slice x32, local copies, waits for them, and re-layouts, elimination(): pivot_imag = work_imag[:, pivot_row, pivot_row]  5.83 us
    dynamic_slice x32, local copies, waits for them, and re-layouts, elimination(): row_imag = work_imag[:, pivot_row, :]  5.66 us
    select_n x2, other arithmetic, per_device(): own_block = jnp.take(coeffs[0, 0], bands, axis=1)  5.31 us
  transfers between devices with their start and end apart: 5, of which 1 were waited for; matrix products, arithmetic and copies ran while one was open for 15% of the time, Pallas kernels for 0%

commit v1 on v0

v1 whole, which is shorter than its diff:
```python
import functools

import jax
import jax.numpy as jnp
from jax import lax
from jax.experimental import pallas as pl
from jax.experimental.pallas import tpu as pltpu
from jax.sharding import PartitionSpec as P

MESH = pl.DeviceIdType.MESH
NB = 32
ROWS = 2 * NB
GX = 128
GY = 256
HALF = GX // 2
EXTRA = 3
CHUNK = 8
NCHUNK = HALF // CHUNK
TILE = 16
F32 = jnp.float32
CONTRACT = (((1,), (1,)), ((), ()))


def dot(a, b):
    return lax.dot_general(a, b, CONTRACT, preferred_element_type=F32)


def complex_parts(square):
    real = square[:NB, :NB] + square[NB:, NB:]
    imag = square[:NB, NB:] - square[NB:, :NB]
    return real, imag


def eliminate(wr, wi):
    lane = lax.broadcasted_iota(jnp.int32, (NB, 128), 1)
    row_id = lax.broadcasted_iota(jnp.int32, (NB, 128), 0)
    base = (lane // NB) * NB
    pivots_r, pivots_i = [], []
    for k in range(NB):
        where = base + k
        col_r = jnp.take_along_axis(wr, where, axis=1)
        col_i = jnp.take_along_axis(wi, where, axis=1)
        pr = col_r[k : k + 1]
        pi = col_i[k : k + 1]
        pivots_r.append(pr)
        pivots_i.append(pi)
        if k == NB - 1:
            break
        mag = pr * pr + pi * pi
        inv_r = pr / mag
        inv_i = -pi / mag
        below = row_id > k
        fr = jnp.where(below, col_r * inv_r - col_i * inv_i, 0.0)
        fi = jnp.where(below, col_r * inv_i + col_i * inv_r, 0.0)
        row_r = wr[k : k + 1]
        row_i = wi[k : k + 1]
        wr, wi = (
            wr - (fr * row_r - fi * row_i),
            wi - (fr * row_i + fi * row_r),
        )
    pr = jnp.concatenate(pivots_r, axis=0)
    pi = jnp.concatenate(pivots_i, axis=0)
    mag = jnp.sqrt(pr * pr + pi * pi)
    ur = pr / mag
    ui = pi / mag
    n = NB
    while n > 1:
        n //= 2
        ar, ai, br, bi = ur[:n], ui[:n], ur[n:], ui[n:]
        ur, ui = ar * br - ai * bi, ar * bi + ai * br
    return ur, ui


def kernel(
    bands, umk, coeffs, out,
    cv, u, zm, zp, xp, xm, szm, szp, sxp, sxm, wb, xb,
    acc_a, acc_b, acc_d, left_src, left_dst, down_src, down_dst,
    unit, unit_x, unit_y,
    load_sem, send_sem, recv_sem, ez_sem, part_sem, unit_sem,
):
    i = lax.axis_index("kx")
    j = lax.axis_index("ky")
    ni = lax.axis_size("kx")
    nj = lax.axis_size("ky")
    right = (lax.rem(i + 1, ni), j)
    left = (lax.rem(i + ni - 1, ni), j)
    up = (i, lax.rem(j + 1, nj))
    down = (i, lax.rem(j + nj - 1, nj))
    x_edge = i == ni - 1
    y_edge = j == 0
    edge = jnp.logical_or(x_edge, y_edge)

    def load(t):
        rows = pl.ds(t * TILE, TILE)
        return pltpu.make_async_copy(coeffs.at[:, :, rows, :], cv[t], load_sem.at[t])

    half_tiles = HALF // TILE
    for t in range(half_tiles):
        load(t).start()
        load(t + half_tiles).start()

    barrier = pltpu.get_barrier_semaphore()
    for device in (right, left, up, down):
        pl.semaphore_signal(barrier, inc=1, device_id=device, device_id_type=MESH)

    zero = jnp.int32(0)
    ax = jnp.where(x_edge, umk[0, 0], zero)
    bx = jnp.where(x_edge, umk[0, 1], zero)
    ay = jnp.where(y_edge, umk[1, 0], zero)
    by = jnp.where(y_edge, umk[1, 1], zero)

    acc_a[...] = jnp.zeros_like(acc_a)
    acc_b[...] = jnp.zeros_like(acc_b)
    acc_d[...] = jnp.zeros_like(acc_d)

    def remote(src, dst, stream, c, device):
        return pltpu.make_async_remote_copy(
            src_ref=src, dst_ref=dst, send_sem=send_sem.at[stream, c],
            recv_sem=recv_sem.at[stream, c], device_id=device, device_id_type=MESH,
        )

    def stream_copy(stream, c, special):
        low = pl.ds(c * CHUNK, CHUNK)
        high = pl.ds(HALF + c * CHUNK, CHUNK)
        own, src, dst, device = (
            (low, szm, zm, down),
            (high, szp, zp, up),
            (low, sxp, xp, right),
            (high, sxm, xm, left),
        )[stream]
        source = src.at[low] if special else u.at[own]
        return remote(source, dst.at[low], stream, c, device)

    need = (y_edge, x_edge, x_edge, y_edge)

    def gather(t):
        rows = pl.ds(t * TILE, TILE)
        parts = [cv[t][r, bands[b]] for r in range(2) for b in range(NB)]
        u[rows] = jnp.swapaxes(jnp.stack(parts, axis=0), 0, 1)

    for t in range(half_tiles):
        load(t).wait()
        gather(t)
        load(t + half_tiles).wait()
        gather(t + half_tiles)
        if t == 0:
            pl.semaphore_wait(barrier, 4)
        for c in range(t * TILE // CHUNK, (t + 1) * TILE // CHUNK):
            for stream in range(4):

                @pl.when(jnp.logical_not(need[stream]))
                def _(stream=stream, c=c):
                    stream_copy(stream, c, False).start()

    def build(dst, count, first, dp, dq):
        shift = lax.rem(GY - dq, GY)

        @pl.loop(0, count)
        def _(p):
            row = lax.rem(first + p + dp + GX, GX)
            dst[p] = pltpu.roll(u[row], shift, 1)

    def build_extra(dst, forward, dq):
        shift = lax.rem(GY - dq, GY)
        for e in range(EXTRA):
            row = jnp.where(forward, e, HALF - EXTRA + e)
            dst[HALF + e] = pltpu.roll(u[row], shift, 1)

    def extra(stream, src, dst, device):
        rows = pl.ds(HALF, EXTRA)
        return pltpu.make_async_remote_copy(
            src_ref=src.at[rows], dst_ref=dst.at[rows], send_sem=ez_sem.at[0, stream],
            recv_sem=ez_sem.at[1, stream], device_id=device, device_id_type=MESH,
        )

    @pl.when(y_edge)
    def _():
        build(szm, HALF, 0, -ay, -by)
        for c in range(NCHUNK):
            stream_copy(0, c, True).start()

    @pl.when(x_edge)
    def _():
        build(szp, HALF, HALF, 0, bx)
        build_extra(szp, ax > 0, bx)
        extra(0, szp, zp, up).start()
        for c in range(NCHUNK):
            stream_copy(1, c, True).start()
        build(sxp, HALF, 0, ax, bx)
        for c in range(NCHUNK):
            stream_copy(2, c, True).start()

    @pl.when(y_edge)
    def _():
        build(sxm, HALF, HALF, 0, -by)
        build_extra(sxm, ay < 0, -by)
        extra(1, sxm, xm, left).start()
        for c in range(NCHUNK):
            stream_copy(3, c, True).start()

    build(wb, HALF, HALF, -ay, bx - by)
    build(xb, HALF, HALF, ax, bx - by)

    @pl.loop(0, NCHUNK)
    def _(c):
        for stream in range(4):
            stream_copy(stream, c, False).wait_recv()
        first = c * CHUNK
        a = None
        b = None
        for q in range(CHUNK):
            p = first + q
            own = u[p]
            lhs = jnp.concatenate([own, xp[p]], axis=0)
            rhs = jnp.concatenate([zm[p], own], axis=0)
            term = dot(lhs, rhs)
            a = term if a is None else a + term
            lhs = jnp.concatenate([zp[p], xb[p]], axis=0)
            rhs = jnp.concatenate([wb[p], xm[p]], axis=0)
            term = dot(lhs, rhs)
            b = term if b is None else b + term
        acc_a[...] += a
        acc_b[...] += b

    acc_d[...] = acc_b[:ROWS, ROWS:]

    @pl.when(x_edge)
    def _():
        extra(0, szp, zp, up).wait_recv()

    @pl.when(y_edge)
    def _():
        extra(1, sxm, xm, left).wait_recv()

    @pl.when(edge)
    def _():
        acc_d[...] = jnp.zeros_like(acc_d)

        @pl.loop(0, HALF // 8)
        def _(c):
            total = None
            for q in range(8):
                s = c * 8 + q + ax
                t = c * 8 + q - ay
                s = jnp.where(s < 0, s + HALF + EXTRA, s)
                t = jnp.where(t < 0, t + HALF + EXTRA, t)
                term = dot(zp[s], xm[t])
                total = term if total is None else total + term
            acc_d[...] += total

    a = acc_a[...]
    b = acc_b[...]
    d_low = complex_parts(a[ROWS:, :ROWS])
    x_low = complex_parts(a[ROWS:, ROWS:])
    y_low = complex_parts(a[:ROWS, :ROWS])
    y_high = complex_parts(b[:ROWS, :ROWS])
    x_high = complex_parts(b[ROWS:, ROWS:])
    d_high = complex_parts(acc_d[...])
    none = jnp.zeros((NB, NB), F32)

    for part in range(2):
        rows = pl.ds(part * NB, NB)
        left_src[rows, :] = jnp.concatenate([x_low[part], none, d_low[part], none], axis=1)
        down_src[rows, :] = jnp.concatenate([none, y_high[part], d_high[part], none], axis=1)

    def part_copy(which):
        src, dst, device = ((left_src, left_dst, left), (down_src, down_dst, down))[which]
        return pltpu.make_async_remote_copy(
            src_ref=src, dst_ref=dst, send_sem=part_sem.at[0, which],
            recv_sem=part_sem.at[1, which], device_id=device, device_id_type=MESH,
        )

    for which in range(2):
        part_copy(which).start()
    own = [
        jnp.concatenate([x_high[part], y_low[part], none, none], axis=1) for part in range(2)
    ]
    for which in range(2):
        part_copy(which).wait_recv()
    wr, wi = (
        own[part] + left_dst[pl.ds(part * NB, NB), :] + down_dst[pl.ds(part * NB, NB), :]
        for part in range(2)
    )
    lane = lax.broadcasted_iota(jnp.int32, (NB, 128), 1)
    unused = lane >= 3 * NB
    wr = jnp.where(unused, 1.0, wr)
    ur, ui = eliminate(wr, wi)
    unit[0:1, :] = ur
    unit[1:2, :] = ui

    def unit_copy(which):
        dst, device = ((unit_x, left), (unit_y, down))[which]
        return pltpu.make_async_remote_copy(
            src_ref=unit, dst_ref=dst, send_sem=unit_sem.at[0, which],
            recv_sem=unit_sem.at[1, which], device_id=device, device_id_type=MESH,
        )

    for which in range(2):
        unit_copy(which).start()
    for which in range(2):
        unit_copy(which).wait_recv()
    out[0:2, :] = unit[0:2, :]
    out[2:4, :] = unit_x[0:2, :]
    out[4:6, :] = unit_y[0:2, :]
    out[6:8, :] = jnp.zeros((2, 128), F32)

    @pl.loop(0, NCHUNK)
    def _(c):
        for stream in range(4):
            stream_copy(stream, c, False).wait_send()

    @pl.when(x_edge)
    def _():
        extra(0, szp, zp, up).wait_send()

    @pl.when(y_edge)
    def _():
        extra(1, sxm, xm, left).wait_send()

    for which in range(2):
        part_copy(which).wait_send()
        unit_copy(which).wait_send()


def times(a, b):
    return a[0] * b[0] - a[1] * b[1], a[0] * b[1] + a[1] * b[0]


def conjugate(a):
    return a[0], -a[1]


def per_device(coeffs, bands, umklapp):
    bf16 = jnp.bfloat16
    half = pltpu.VMEM((HALF, ROWS, GY), bf16)
    longer = pltpu.VMEM((HALF + EXTRA, ROWS, GY), bf16)
    table = pl.pallas_call(
        kernel,
        out_shape=jax.ShapeDtypeStruct((8, 128), F32),
        in_specs=[
            pl.BlockSpec(memory_space=pltpu.SMEM),
            pl.BlockSpec(memory_space=pltpu.SMEM),
            pl.BlockSpec(memory_space=pl.ANY),
        ],
        out_specs=pl.BlockSpec(memory_space=pltpu.VMEM),
        scratch_shapes=[
            [pltpu.VMEM((*coeffs.shape[2:4], TILE, GY), bf16)] * (GX // TILE),
            pltpu.VMEM((GX, ROWS, GY), bf16),
            half, longer, half, longer,
            half, longer, half, longer, half, half,
            pltpu.VMEM((2 * ROWS, 2 * ROWS), F32),
            pltpu.VMEM((2 * ROWS, 2 * ROWS), F32),
            pltpu.VMEM((ROWS, ROWS), F32),
            pltpu.VMEM((ROWS, 128), F32),
            pltpu.VMEM((ROWS, 128), F32),
            pltpu.VMEM((ROWS, 128), F32),
            pltpu.VMEM((ROWS, 128), F32),
            pltpu.VMEM((8, 128), F32),
            pltpu.VMEM((8, 128), F32),
            pltpu.VMEM((8, 128), F32),
            pltpu.SemaphoreType.DMA((GX // TILE,)),
            pltpu.SemaphoreType.DMA((4, NCHUNK)),
            pltpu.SemaphoreType.DMA((4, NCHUNK)),
            pltpu.SemaphoreType.DMA((2, 2)),
            pltpu.SemaphoreType.DMA((2, 2)),
            pltpu.SemaphoreType.DMA((2, 2)),
        ],
        compiler_params=pltpu.CompilerParams(
            collective_id=0, has_side_effects=True, vmem_limit_bytes=56 << 20
        ),
    )(bands, umklapp, coeffs[0, 0])

    def link(row, which):
        return table[row, which * NB], table[row + 1, which * NB]

    along_x, along_y, along_d = (link(0, which) for which in range(3))
    y_next = link(2, 1)
    x_next = link(4, 0)
    first = times(times(along_x, y_next), conjugate(along_d))
    second = times(times(along_d, conjugate(x_next)), conjugate(along_y))
    flux = jnp.stack([jnp.arctan2(first[1], first[0]), jnp.arctan2(second[1], second[0])])
    links = jnp.stack([*along_x, *along_y, *along_d])
    return flux.reshape(1, 1, 2), links.reshape(1, 1, 3, 2)


def solution(mesh):
    in_specs = (P("kx", "ky", None, None, None, None), P(), P())
    out_specs = (P("kx", "ky", None), P("kx", "ky", None, None))
    return jax.shard_map(
        per_device, mesh=mesh, in_specs=in_specs, out_specs=out_specs, check_vma=False
    )
```

time: 265 us -> 113 us (0.43)
  the two profiles are of different devices: /device:TPU:1 before, /device:TPU:215 now
where the time goes in v1:
time: 113 us; the launch traced here: 112 us
  Pallas kernels  91.5 us (81%)
  between operations  13.9 us (12%)
  local copies, waits for them, and re-layouts  6.23 us (6%)
    pallas_call x1, Pallas kernels, per_device(): pl.pallas_call(kernel, out_shape=jax.ShapeDtypeStruct((8, 128), F32), in_...  91.5 us
    another operation x1, local copies, waits for them, and re-layouts, per_device(): links = jnp.stack([*along_x, *along_y, *along_d])  3.77 us

profile of v1, /device:TPU:215, one launch (start us, length us, event | category | flops | bytes accessed | tf_op | source)
XLA Modules:
  0.0 112.2 jit_solution(10150752356140387929)
XLA Ops:
  0.6 91.5 %shard_map.50 = f32[8,128]{1,0:T(8,128)} custom-call(s32[32]{0:T(128)} %bands.1, s32[2,2]{1,0:T(2,128)} %umk.1, bf16[2,36,128,256]{3,2,1,0:T(8,128)(2,1)} %bitcast.19), custom_call_target="tpu_custom_call" | custom-call | tf_op jit(solution)/shard_map/pallas_call | solution.py:337
  92.2 1.7 %fusion = (f32[1,1]{1,0:T(1,128)}, f32[1,1]{1,0:T(1,128)}, f32[1,1]{1,0:T(1,128)}, f32[1,1]{1,0:T(1,128)}, f32[1,1]{1,0:T(1,128)}, /*index=5*/f32[1,1]{1,0:T(1,1...) fusion(f32[8,128]{1,0:T(8,128)} %shard_map.50), kind=kLoop, calls=%fused_computation.1 | loop fusion | bytes 80 | tf_op jit(solution)/shard_map/slice | solution.py:374
  107.1 0.6 maximum_bitcast_fusion
  107.7 3.8 %stack.15 = f32[6]{0:T(128)S(1)} concatenate(f32[1]{0:T(128)} %bitcast.12, f32[1]{0:T(128)} %bitcast.13, f32[1]{0:T(128)} %bitcast.14, f32[1]{0:T(128)} %bitcast.15, f32[1]{0:T(128)} %bitcast.16, f32[1]{0:T(128)} %bitcast.17), dimensions={0} | concatenate | bytes 48 | tf_op jit(solution)/shard_map/stack | solution.py:382
  111.5 0.1 reshape.19
  111.6 0.7 copy.6

commit v2 on v1

--- a/solution.py
+++ b/solution.py
@@ -29,6 +29,14 @@
     real = square[:NB, :NB] + square[NB:, NB:]
     imag = square[:NB, NB:] - square[NB:, :NB]
     return real, imag
+
+
+def times(a, b):
+    return a[0] * b[0] - a[1] * b[1], a[0] * b[1] + a[1] * b[0]
+
+
+def conjugate(a):
+    return a[0], -a[1]
 
 
 def eliminate(wr, wi):
@@ -72,8 +80,8 @@
 
 
 def kernel(
-    bands, umk, coeffs, out,
-    cv, u, zm, zp, xp, xm, szm, szp, sxp, sxm, wb, xb,
+    bands, umk, coeffs, flux, links,
+    cv, perm, u, zm, zp, xp, xm, szm, szp, sxp, sxm, wb, xb,
     acc_a, acc_b, acc_d, left_src, left_dst, down_src, down_dst,
     unit, unit_x, unit_y,
     load_sem, send_sem, recv_sem, ez_sem, part_sem, unit_sem,
@@ -109,6 +117,12 @@
     ay = jnp.where(y_edge, umk[1, 0], zero)
     by = jnp.where(y_edge, umk[1, 1], zero)
 
+    size = TILE * TILE
+    to = lax.broadcasted_iota(jnp.int32, (size, size), 0)
+    take = lax.broadcasted_iota(jnp.int32, (size, size), 1)
+    swap = (to % TILE) * TILE + to // TILE
+    perm[...] = jnp.where(take == swap, 1.0, 0.0).astype(jnp.bfloat16)
+
     acc_a[...] = jnp.zeros_like(acc_a)
     acc_b[...] = jnp.zeros_like(acc_b)
     acc_d[...] = jnp.zeros_like(acc_d)
@@ -135,8 +149,12 @@
 
     def gather(t):
         rows = pl.ds(t * TILE, TILE)
-        parts = [cv[t][r, bands[b]] for r in range(2) for b in range(NB)]
-        u[rows] = jnp.swapaxes(jnp.stack(parts, axis=0), 0, 1)
+        for g in range(ROWS // TILE):
+            r, b = divmod(g * TILE, NB)
+            parts = [cv[t][r, bands[b + e]] for e in range(TILE)]
+            moved = jnp.dot(perm[...], jnp.concatenate(parts, axis=0), preferred_element_type=F32)
+            moved = moved.astype(jnp.bfloat16).reshape(TILE, TILE, GY)
+            u[rows, pl.ds(g * TILE, TILE), :] = moved
 
     for t in range(half_tiles):
         load(t).wait()
@@ -155,10 +173,12 @@
     def build(dst, count, first, dp, dq):
         shift = lax.rem(GY - dq, GY)
 
-        @pl.loop(0, count)
-        def _(p):
-            row = lax.rem(first + p + dp + GX, GX)
-            dst[p] = pltpu.roll(u[row], shift, 1)
+        @pl.loop(0, count // 8)
+        def _(c):
+            for q in range(8):
+                p = c * 8 + q
+                row = lax.rem(first + p + dp + GX, GX)
+                dst[p] = pltpu.roll(u[row], shift, 1)
 
     def build_extra(dst, forward, dq):
         shift = lax.rem(GY - dq, GY)
@@ -299,10 +319,29 @@
         unit_copy(which).start()
     for which in range(2):
         unit_copy(which).wait_recv()
-    out[0:2, :] = unit[0:2, :]
-    out[2:4, :] = unit_x[0:2, :]
-    out[4:6, :] = unit_y[0:2, :]
-    out[6:8, :] = jnp.zeros((2, 128), F32)
+
+    def group(ref, which):
+        real, imag = ref[0:1, :], ref[1:2, :]
+        if which:
+            shift = 128 - which * NB
+            real, imag = pltpu.roll(real, shift, 1), pltpu.roll(imag, shift, 1)
+        return real, imag
+
+    along_x, along_y, along_d = (group(unit, which) for which in range(3))
+    y_next = group(unit_x, 1)
+    x_next = group(unit_y, 0)
+    first = times(times(along_x, y_next), conjugate(along_d))
+    second = times(times(along_d, conjugate(x_next)), conjugate(along_y))
+    is_real = lax.broadcasted_iota(jnp.int32, (1, 128), 1) == 0
+    angle = jnp.arctan2(
+        jnp.where(is_real, first[1], second[1]), jnp.where(is_real, first[0], second[0])
+    )
+    flux[0] = angle[:, :2]
+    lane = lax.broadcasted_iota(jnp.int32, (1, 128), 1)
+    for part in range(2):
+        row = jnp.where(lane == 0, along_x[part], along_y[part])
+        row = jnp.where(lane == 2, along_d[part], row)
+        links[0, 0, part : part + 1, :] = row[:, :3]
 
     @pl.loop(0, NCHUNK)
     def _(c):
@@ -322,29 +361,25 @@
         unit_copy(which).wait_send()
 
 
-def times(a, b):
-    return a[0] * b[0] - a[1] * b[1], a[0] * b[1] + a[1] * b[0]
-
-
-def conjugate(a):
-    return a[0], -a[1]
-
-
 def per_device(coeffs, bands, umklapp):
     bf16 = jnp.bfloat16
     half = pltpu.VMEM((HALF, ROWS, GY), bf16)
     longer = pltpu.VMEM((HALF + EXTRA, ROWS, GY), bf16)
-    table = pl.pallas_call(
+    flux, links = pl.pallas_call(
         kernel,
-        out_shape=jax.ShapeDtypeStruct((8, 128), F32),
+        out_shape=(
+            jax.ShapeDtypeStruct((1, 1, 2), F32),
+            jax.ShapeDtypeStruct((1, 1, 2, 3), F32),
+        ),
         in_specs=[
             pl.BlockSpec(memory_space=pltpu.SMEM),
             pl.BlockSpec(memory_space=pltpu.SMEM),
             pl.BlockSpec(memory_space=pl.ANY),
         ],
-        out_specs=pl.BlockSpec(memory_space=pltpu.VMEM),
+        out_specs=(pl.BlockSpec(memory_space=pltpu.VMEM),) * 2,
         scratch_shapes=[
             [pltpu.VMEM((*coeffs.shape[2:4], TILE, GY), bf16)] * (GX // TILE),
+            pltpu.VMEM((TILE * TILE, TILE * TILE), bf16),
             pltpu.VMEM((GX, ROWS, GY), bf16),
             half, longer, half, longer,
             half, longer, half, longer, half, half,
@@ -369,18 +404,7 @@
             collective_id=0, has_side_effects=True, vmem_limit_bytes=56 << 20
         ),
     )(bands, umklapp, coeffs[0, 0])
-
-    def link(row, which):
-        return table[row, which * NB], table[row + 1, which * NB]
-
-    along_x, along_y, along_d = (link(0, which) for which in range(3))
-    y_next = link(2, 1)
-    x_next = link(4, 0)
-    first = times(times(along_x, y_next), conjugate(along_d))
-    second = times(times(along_d, conjugate(x_next)), conjugate(along_y))
-    flux = jnp.stack([jnp.arctan2(first[1], first[0]), jnp.arctan2(second[1], second[0])])
-    links = jnp.stack([*along_x, *along_y, *along_d])
-    return flux.reshape(1, 1, 2), links.reshape(1, 1, 3, 2)
+    return flux, jnp.swapaxes(links, 2, 3)
 
 
 def solution(mesh):

time: 113 us -> 93.4 us (0.83)
  the two profiles are of different devices: /device:TPU:215 before, /device:TPU:29 now
where the time goes in v2:
time: 93.4 us; the launch traced here: 93.2 us
  Pallas kernels  90.2 us (97%)
  local copies, waits for them, and re-layouts  2.36 us (3%)
    pallas_call x1, Pallas kernels, per_device(): pl.pallas_call(kernel, out_shape=(jax.ShapeDtypeStruct((1, 1, 2), F32), j...  90.2 us
    unnamed x2, local copies, waits for them, and re-layouts  2.36 us

profile of v2, /device:TPU:29, one launch (start us, length us, event | category | flops | bytes accessed | tf_op | source)
XLA Modules:
  0.0 93.2 jit_solution(16683103452206984624)
XLA Ops:
  0.6 90.2 %shard_map.50 = (f32[1,1,2]{2,1,0:T(1,128)}, f32[1,1,2,3]{3,2,1,0:T(2,128)}) custom-call(s32[32]{0:T(128)} %bands.1, s32[2,2]{1,0:T(2,128)} %umk.1, bf16[2,36,128,256]{3,2,1,0:T(8,128)(2,1)} %bitcast.2), custom_call_target="tpu_custom_call" | custom-call | tf_op jit(solution)/shard_map/pallas_call | solution.py:368
  90.9 1.1 %copy.7 = f32[1,1,2]{2,1,0:T(1,128)} copy(f32[1,1,2]{2,1,0:T(1,128)} %get-tuple-element.8) | data formatting | bytes 16
  92.0 1.2 %copy.8 = f32[1,1,3,2]{2,3,1,0:T(2,128)} copy(f32[1,1,3,2]{2,3,1,0:T(2,128)} %bitcast.3) | data formatting | bytes 48

commit v3 on v2

--- a/solution.py
+++ b/solution.py
@@ -17,6 +17,8 @@
 CHUNK = 8
 NCHUNK = HALF // CHUNK
 TILE = 16
+GROUP = 8
+RELAYED = (1, 1, 4, 4)
 F32 = jnp.float32
 CONTRACT = (((1,), (1,)), ((), ()))
 
@@ -84,7 +86,7 @@
     cv, perm, u, zm, zp, xp, xm, szm, szp, sxp, sxm, wb, xb,
     acc_a, acc_b, acc_d, left_src, left_dst, down_src, down_dst,
     unit, unit_x, unit_y,
-    load_sem, send_sem, recv_sem, ez_sem, part_sem, unit_sem,
+    hop, load_sem, send_sem, recv_sem, ez_sem, part_sem, unit_sem, hop_sem,
 ):
     i = lax.axis_index("kx")
     j = lax.axis_index("ky")
@@ -107,9 +109,50 @@
         load(t).start()
         load(t + half_tiles).start()
 
+    def shifted(di, dj):
+        return lax.rem(i + di + ni, ni), lax.rem(j + dj + nj, nj)
+
+    in_row = lax.rem(i, GROUP)
+    in_column = lax.rem(j, GROUP)
+    first_plane = in_column == 0
+    last_plane = in_column == GROUP - 1
+    wrap_plane = jnp.logical_or(first_plane, last_plane)
+    sends_by = (
+        first_plane,
+        last_plane,
+        jnp.logical_and(wrap_plane, in_row == GROUP - 1),
+        jnp.logical_and(wrap_plane, in_row == 0),
+    )
+    relay_of = (shifted(0, -2), shifted(0, 2), shifted(6, 0), shifted(-6, 0))
+    is_relay = (
+        in_column == GROUP - 2,
+        in_column == 1,
+        jnp.logical_and(wrap_plane, in_row == 5),
+        jnp.logical_and(wrap_plane, in_row == 2),
+    )
+    relay_from = (shifted(0, 2), shifted(0, -2), shifted(-6, 0), shifted(6, 0))
+    relay_to = (up, down, shifted(-5, 0), shifted(5, 0))
+    gets_by = (None, None, sends_by[3], sends_by[2])
+    gets_from = (None, None, shifted(5, 0), shifted(-5, 0))
+
     barrier = pltpu.get_barrier_semaphore()
     for device in (right, left, up, down):
         pl.semaphore_signal(barrier, inc=1, device_id=device, device_id_type=MESH)
+    arrivals = jnp.int32(4)
+    for flags, devices in (
+        (sends_by, relay_of),
+        (is_relay, relay_from),
+        ((None, None, *is_relay[2:]), relay_to),
+        (gets_by, gets_from),
+    ):
+        for flag, device in zip(flags, devices, strict=True):
+            if flag is None:
+                continue
+            arrivals = arrivals + jnp.where(flag, 1, 0)
+
+            @pl.when(flag)
+            def _(device=device):
+                pl.semaphore_signal(barrier, inc=1, device_id=device, device_id_type=MESH)
 
     zero = jnp.int32(0)
     ax = jnp.where(x_edge, umk[0, 0], zero)
@@ -133,7 +176,7 @@
             recv_sem=recv_sem.at[stream, c], device_id=device, device_id_type=MESH,
         )
 
-    def stream_copy(stream, c, special):
+    def stream_ends(stream, c, special):
         low = pl.ds(c * CHUNK, CHUNK)
         high = pl.ds(HALF + c * CHUNK, CHUNK)
         own, src, dst, device = (
@@ -143,7 +186,48 @@
             (high, sxm, xm, left),
         )[stream]
         source = src.at[low] if special else u.at[own]
-        return remote(source, dst.at[low], stream, c, device)
+        return source, dst.at[low], device
+
+    def stream_wait(stream, c):
+        return remote(*stream_ends(stream, c, False)[:2], stream, c, right)
+
+    def stream_send(stream, c, special, when):
+        source, target, device = stream_ends(stream, c, special)
+        if c >= RELAYED[stream]:
+
+            @pl.when(when)
+            def _():
+                remote(source, target, stream, c, device).start()
+
+            return
+
+        @pl.when(jnp.logical_and(when, jnp.logical_not(sends_by[stream])))
+        def _():
+            remote(source, target, stream, c, device).start()
+
+        @pl.when(jnp.logical_and(when, sends_by[stream]))
+        def _():
+            pltpu.make_async_remote_copy(
+                src_ref=source, dst_ref=hop.at[pl.ds(c * CHUNK, CHUNK)],
+                send_sem=send_sem.at[stream, c], recv_sem=hop_sem.at[0, c],
+                device_id=relay_of[stream], device_id_type=MESH,
+            ).start()
+
+    def relay_copy(stream, c):
+        source = hop.at[pl.ds(c * CHUNK, CHUNK)]
+        target = stream_ends(stream, c, False)[1]
+        return pltpu.make_async_remote_copy(
+            src_ref=source, dst_ref=target, send_sem=hop_sem.at[1, c],
+            recv_sem=recv_sem.at[stream, c], device_id=relay_to[stream],
+            device_id_type=MESH,
+        )
+
+    def relay_arrival(c):
+        rows = hop.at[pl.ds(c * CHUNK, CHUNK)]
+        return pltpu.make_async_remote_copy(
+            src_ref=rows, dst_ref=rows, send_sem=hop_sem.at[1, c],
+            recv_sem=hop_sem.at[0, c], device_id=right, device_id_type=MESH,
+        )
 
     need = (y_edge, x_edge, x_edge, y_edge)
 
@@ -162,13 +246,10 @@
         load(t + half_tiles).wait()
         gather(t + half_tiles)
         if t == 0:
-            pl.semaphore_wait(barrier, 4)
+            pl.semaphore_wait(barrier, arrivals)
         for c in range(t * TILE // CHUNK, (t + 1) * TILE // CHUNK):
             for stream in range(4):
-
-                @pl.when(jnp.logical_not(need[stream]))
-                def _(stream=stream, c=c):
-                    stream_copy(stream, c, False).start()
+                stream_send(stream, c, False, jnp.logical_not(need[stream]))
 
     def build(dst, count, first, dp, dq):
         shift = lax.rem(GY - dq, GY)
@@ -197,7 +278,7 @@
     def _():
         build(szm, HALF, 0, -ay, -by)
         for c in range(NCHUNK):
-            stream_copy(0, c, True).start()
+            stream_send(0, c, True, True)
 
     @pl.when(x_edge)
     def _():
@@ -205,10 +286,10 @@
         build_extra(szp, ax > 0, bx)
         extra(0, szp, zp, up).start()
         for c in range(NCHUNK):
-            stream_copy(1, c, True).start()
+            stream_send(1, c, True, True)
         build(sxp, HALF, 0, ax, bx)
         for c in range(NCHUNK):
-            stream_copy(2, c, True).start()
+            stream_send(2, c, True, True)
 
     @pl.when(y_edge)
     def _():
@@ -216,7 +297,15 @@
         build_extra(sxm, ay < 0, -by)
         extra(1, sxm, xm, left).start()
         for c in range(NCHUNK):
-            stream_copy(3, c, True).start()
+            stream_send(3, c, True, True)
+
+    for stream in range(4):
+
+        @pl.when(is_relay[stream])
+        def _(stream=stream):
+            for c in range(RELAYED[stream]):
+                relay_arrival(c).wait_recv()
+                relay_copy(stream, c).start()
 
     build(wb, HALF, HALF, -ay, bx - by)
     build(xb, HALF, HALF, ax, bx - by)
@@ -224,7 +313,7 @@
     @pl.loop(0, NCHUNK)
     def _(c):
         for stream in range(4):
-            stream_copy(stream, c, False).wait_recv()
+            stream_wait(stream, c).wait_recv()
         first = c * CHUNK
         a = None
         b = None
@@ -346,7 +435,7 @@
     @pl.loop(0, NCHUNK)
     def _(c):
         for stream in range(4):
-            stream_copy(stream, c, False).wait_send()
+            stream_wait(stream, c).wait_send()
 
     @pl.when(x_edge)
     def _():
@@ -355,6 +444,13 @@
     @pl.when(y_edge)
     def _():
         extra(1, sxm, xm, left).wait_send()
+
+    for stream in range(4):
+
+        @pl.when(is_relay[stream])
+        def _(stream=stream):
+            for c in range(RELAYED[stream]):
+                relay_copy(stream, c).wait_send()
 
     for which in range(2):
         part_copy(which).wait_send()
@@ -393,12 +489,14 @@
             pltpu.VMEM((8, 128), F32),
             pltpu.VMEM((8, 128), F32),
             pltpu.VMEM((8, 128), F32),
+            pltpu.VMEM((max(RELAYED) * CHUNK, ROWS, GY), bf16),
             pltpu.SemaphoreType.DMA((GX // TILE,)),
             pltpu.SemaphoreType.DMA((4, NCHUNK)),
             pltpu.SemaphoreType.DMA((4, NCHUNK)),
             pltpu.SemaphoreType.DMA((2, 2)),
             pltpu.SemaphoreType.DMA((2, 2)),
             pltpu.SemaphoreType.DMA((2, 2)),
+            pltpu.SemaphoreType.DMA((2, max(RELAYED))),
         ],
         compiler_params=pltpu.CompilerParams(
             collective_id=0, has_side_effects=True, vmem_limit_bytes=56 << 20

time: 93.4 us -> 80.7 us (0.86)
  the two profiles are of different devices: /device:TPU:29 before, /device:TPU:1 now
where the time goes in v3:
time: 80.7 us; the launch traced here: 79.7 us
  Pallas kernels  76.7 us (95%)
  local copies, waits for them, and re-layouts  2.36 us (3%)
    pallas_call x1, Pallas kernels, per_device(): pl.pallas_call(kernel, out_shape=(jax.ShapeDtypeStruct((1, 1, 2), F32), j...  76.7 us
    unnamed x2, local copies, waits for them, and re-layouts  2.36 us

profile of v3, /device:TPU:1, one launch (start us, length us, event | category | flops | bytes accessed | tf_op | source)
XLA Modules:
  0.0 79.7 jit_solution(6765956479361298830)
XLA Ops:
  0.6 76.7 %shard_map.50 = (f32[1,1,2]{2,1,0:T(1,128)}, f32[1,1,2,3]{3,2,1,0:T(2,128)}) custom-call(s32[32]{0:T(128)} %bands.1, s32[2,2]{1,0:T(2,128)} %umk.1, bf16[2,36,128,256]{3,2,1,0:T(8,128)(2,1)} %bitcast.2), custom_call_target="tpu_custom_call" | custom-call | tf_op jit(solution)/shard_map/pallas_call | solution.py:464
  77.3 1.1 %copy.7 = f32[1,1,2]{2,1,0:T(1,128)} copy(f32[1,1,2]{2,1,0:T(1,128)} %get-tuple-element.8) | data formatting | bytes 16
  78.5 1.2 %copy.8 = f32[1,1,3,2]{2,3,1,0:T(2,128)} copy(f32[1,1,3,2]{2,3,1,0:T(2,128)} %bitcast.3) | data formatting | bytes 48

commit v4 on v3

--- a/solution.py
+++ b/solution.py
@@ -18,7 +18,8 @@
 NCHUNK = HALF // CHUNK
 TILE = 16
 GROUP = 8
-RELAYED = (1, 1, 4, 4)
+RELAYED = ((1,), (1,), (4, 5, 6, 7), (4, 5, 6, 7))
+LATE = 4
 F32 = jnp.float32
 CONTRACT = (((1,), (1,)), ((), ()))
 
@@ -105,9 +106,8 @@
         return pltpu.make_async_copy(coeffs.at[:, :, rows, :], cv[t], load_sem.at[t])
 
     half_tiles = HALF // TILE
-    for t in range(half_tiles):
-        load(t).start()
-        load(t + half_tiles).start()
+    load(0).start()
+    load(half_tiles).start()
 
     def shifted(di, dj):
         return lax.rem(i + di + ni, ni), lax.rem(j + dj + nj, nj)
@@ -123,17 +123,17 @@
         jnp.logical_and(wrap_plane, in_row == GROUP - 1),
         jnp.logical_and(wrap_plane, in_row == 0),
     )
-    relay_of = (shifted(0, -2), shifted(0, 2), shifted(6, 0), shifted(-6, 0))
+    relay_of = (shifted(0, -2), shifted(0, 2), shifted(5, 0), shifted(-5, 0))
     is_relay = (
         in_column == GROUP - 2,
         in_column == 1,
-        jnp.logical_and(wrap_plane, in_row == 5),
-        jnp.logical_and(wrap_plane, in_row == 2),
+        jnp.logical_and(wrap_plane, in_row == 4),
+        jnp.logical_and(wrap_plane, in_row == 3),
     )
-    relay_from = (shifted(0, 2), shifted(0, -2), shifted(-6, 0), shifted(6, 0))
-    relay_to = (up, down, shifted(-5, 0), shifted(5, 0))
+    relay_from = (shifted(0, 2), shifted(0, -2), shifted(-5, 0), shifted(5, 0))
+    relay_to = (up, down, shifted(-4, 0), shifted(4, 0))
     gets_by = (None, None, sends_by[3], sends_by[2])
-    gets_from = (None, None, shifted(5, 0), shifted(-5, 0))
+    gets_from = (None, None, shifted(4, 0), shifted(-4, 0))
 
     barrier = pltpu.get_barrier_semaphore()
     for device in (right, left, up, down):
@@ -170,6 +170,10 @@
     acc_b[...] = jnp.zeros_like(acc_b)
     acc_d[...] = jnp.zeros_like(acc_d)
 
+    for t in range(1, half_tiles):
+        load(t).start()
+        load(t + half_tiles).start()
+
     def remote(src, dst, stream, c, device):
         return pltpu.make_async_remote_copy(
             src_ref=src, dst_ref=dst, send_sem=send_sem.at[stream, c],
@@ -188,12 +192,17 @@
         source = src.at[low] if special else u.at[own]
         return source, dst.at[low], device
 
+    def slot(stream, c):
+        return pl.ds(RELAYED[stream].index(c) * CHUNK, CHUNK)
+
     def stream_wait(stream, c):
         return remote(*stream_ends(stream, c, False)[:2], stream, c, right)
 
-    def stream_send(stream, c, special, when):
+    def stream_send(stream, c, special, when, first=False):
         source, target, device = stream_ends(stream, c, special)
-        if c >= RELAYED[stream]:
+        if first and stream < 2 and c >= LATE:
+            when = jnp.logical_and(when, jnp.logical_not(is_relay[1 - stream]))
+        if c not in RELAYED[stream]:
 
             @pl.when(when)
             def _():
@@ -208,13 +217,13 @@
         @pl.when(jnp.logical_and(when, sends_by[stream]))
         def _():
             pltpu.make_async_remote_copy(
-                src_ref=source, dst_ref=hop.at[pl.ds(c * CHUNK, CHUNK)],
+                src_ref=source, dst_ref=hop.at[slot(stream, c)],
                 send_sem=send_sem.at[stream, c], recv_sem=hop_sem.at[0, c],
                 device_id=relay_of[stream], device_id_type=MESH,
             ).start()
 
     def relay_copy(stream, c):
-        source = hop.at[pl.ds(c * CHUNK, CHUNK)]
+        source = hop.at[slot(stream, c)]
         target = stream_ends(stream, c, False)[1]
         return pltpu.make_async_remote_copy(
             src_ref=source, dst_ref=target, send_sem=hop_sem.at[1, c],
@@ -222,8 +231,8 @@
             device_id_type=MESH,
         )
 
-    def relay_arrival(c):
-        rows = hop.at[pl.ds(c * CHUNK, CHUNK)]
+    def relay_arrival(stream, c):
+        rows = hop.at[slot(stream, c)]
         return pltpu.make_async_remote_copy(
             src_ref=rows, dst_ref=rows, send_sem=hop_sem.at[1, c],
             recv_sem=hop_sem.at[0, c], device_id=right, device_id_type=MESH,
@@ -249,7 +258,7 @@
             pl.semaphore_wait(barrier, arrivals)
         for c in range(t * TILE // CHUNK, (t + 1) * TILE // CHUNK):
             for stream in range(4):
-                stream_send(stream, c, False, jnp.logical_not(need[stream]))
+                stream_send(stream, c, False, jnp.logical_not(need[stream]), True)
 
     def build(dst, count, first, dp, dq):
         shift = lax.rem(GY - dq, GY)
@@ -278,7 +287,7 @@
     def _():
         build(szm, HALF, 0, -ay, -by)
         for c in range(NCHUNK):
-            stream_send(0, c, True, True)
+            stream_send(0, c, True, True, True)
 
     @pl.when(x_edge)
     def _():
@@ -286,10 +295,10 @@
         build_extra(szp, ax > 0, bx)
         extra(0, szp, zp, up).start()
         for c in range(NCHUNK):
-            stream_send(1, c, True, True)
+            stream_send(1, c, True, True, True)
         build(sxp, HALF, 0, ax, bx)
         for c in range(NCHUNK):
-            stream_send(2, c, True, True)
+            stream_send(2, c, True, True, True)
 
     @pl.when(y_edge)
     def _():
@@ -297,21 +306,29 @@
         build_extra(sxm, ay < 0, -by)
         extra(1, sxm, xm, left).start()
         for c in range(NCHUNK):
-            stream_send(3, c, True, True)
+            stream_send(3, c, True, True, True)
 
     for stream in range(4):
 
         @pl.when(is_relay[stream])
         def _(stream=stream):
-            for c in range(RELAYED[stream]):
-                relay_arrival(c).wait_recv()
+            for c in RELAYED[stream]:
+                relay_arrival(stream, c).wait_recv()
                 relay_copy(stream, c).start()
+            if stream < 2:
+                other = 1 - stream
+                for c in range(LATE, NCHUNK):
+                    stream_send(other, c, False, jnp.logical_not(need[other]))
+                    stream_send(other, c, True, need[other])
 
     build(wb, HALF, HALF, -ay, bx - by)
     build(xb, HALF, HALF, ax, bx - by)
 
     @pl.loop(0, NCHUNK)
-    def _(c):
+    def _(step):
+        early, late = RELAYED[0][0], len(RELAYED[0])
+        c = jnp.where(step < early, step, step + late)
+        c = jnp.where(step < NCHUNK - late, c, early + step - (NCHUNK - late))
         for stream in range(4):
             stream_wait(stream, c).wait_recv()
         first = c * CHUNK
@@ -345,12 +362,12 @@
     def _():
         acc_d[...] = jnp.zeros_like(acc_d)
 
-        @pl.loop(0, HALF // 8)
+        @pl.loop(0, HALF // 32)
         def _(c):
             total = None
-            for q in range(8):
-                s = c * 8 + q + ax
-                t = c * 8 + q - ay
+            for q in range(32):
+                s = c * 32 + q + ax
+                t = c * 32 + q - ay
                 s = jnp.where(s < 0, s + HALF + EXTRA, s)
                 t = jnp.where(t < 0, t + HALF + EXTRA, t)
                 term = dot(zp[s], xm[t])
@@ -449,7 +466,7 @@
 
         @pl.when(is_relay[stream])
         def _(stream=stream):
-            for c in range(RELAYED[stream]):
+            for c in RELAYED[stream]:
                 relay_copy(stream, c).wait_send()
 
     for which in range(2):
@@ -489,14 +506,14 @@
             pltpu.VMEM((8, 128), F32),
             pltpu.VMEM((8, 128), F32),
             pltpu.VMEM((8, 128), F32),
-            pltpu.VMEM((max(RELAYED) * CHUNK, ROWS, GY), bf16),
+            pltpu.VMEM((max(map(len, RELAYED)) * CHUNK, ROWS, GY), bf16),
             pltpu.SemaphoreType.DMA((GX // TILE,)),
             pltpu.SemaphoreType.DMA((4, NCHUNK)),
             pltpu.SemaphoreType.DMA((4, NCHUNK)),
             pltpu.SemaphoreType.DMA((2, 2)),
             pltpu.SemaphoreType.DMA((2, 2)),
             pltpu.SemaphoreType.DMA((2, 2)),
-            pltpu.SemaphoreType.DMA((2, max(RELAYED))),
+            pltpu.SemaphoreType.DMA((2, NCHUNK)),
         ],
         compiler_params=pltpu.CompilerParams(
             collective_id=0, has_side_effects=True, vmem_limit_bytes=56 << 20

time: 80.7 us -> 78.1 us (0.968); the launches traced: 79.7 us -> 77.9 us
  Pallas kernels: 76.7 us -> 74.9 us
    pallas_call x1, Pallas kernels: 76.7 us -> 74.9 us  [per_device(): pl.pallas_call(kernel, out_shape=(jax.ShapeDtypeStruct((1, 1, 2), F32), j...]
where the time goes in v4:
time: 78.1 us; the launch traced here: 77.9 us
  Pallas kernels  74.9 us (96%)
  local copies, waits for them, and re-layouts  2.36 us (3%)
    pallas_call x1, Pallas kernels, per_device(): pl.pallas_call(kernel, out_shape=(jax.ShapeDtypeStruct((1, 1, 2), F32), j...  74.9 us
    unnamed x2, local copies, waits for them, and re-layouts  2.36 us

profile of v4, /device:TPU:1, one launch (start us, length us, event | category | flops | bytes accessed | tf_op | source)
XLA Modules:
  0.0 77.9 jit_solution(10971704115491015205)
XLA Ops:
  0.6 74.9 %shard_map.50 = (f32[1,1,2]{2,1,0:T(1,128)}, f32[1,1,2,3]{3,2,1,0:T(2,128)}) custom-call(s32[32]{0:T(128)} %bands.1, s32[2,2]{1,0:T(2,128)} %umk.1, bf16[2,36,128,256]{3,2,1,0:T(8,128)(2,1)} %bitcast.2), custom_call_target="tpu_custom_call" | custom-call | tf_op jit(solution)/shard_map/pallas_call | solution.py:481
  75.6 1.1 %copy.7 = f32[1,1,2]{2,1,0:T(1,128)} copy(f32[1,1,2]{2,1,0:T(1,128)} %get-tuple-element.8) | data formatting | bytes 16
  76.7 1.2 %copy.8 = f32[1,1,3,2]{2,3,1,0:T(2,128)} copy(f32[1,1,3,2]{2,3,1,0:T(2,128)} %bitcast.3) | data formatting | bytes 48

commit v5 on v4

--- a/solution.py
+++ b/solution.py
@@ -42,35 +42,39 @@
     return a[0], -a[1]
 
 
-def eliminate(wr, wi):
+def eliminate(tiles):
     lane = lax.broadcasted_iota(jnp.int32, (NB, 128), 1)
     row_id = lax.broadcasted_iota(jnp.int32, (NB, 128), 0)
     base = (lane // NB) * NB
-    pivots_r, pivots_i = [], []
+    tiles = list(tiles)
+    pivots = [([], []) for _ in tiles]
     for k in range(NB):
         where = base + k
-        col_r = jnp.take_along_axis(wr, where, axis=1)
-        col_i = jnp.take_along_axis(wi, where, axis=1)
-        pr = col_r[k : k + 1]
-        pi = col_i[k : k + 1]
-        pivots_r.append(pr)
-        pivots_i.append(pi)
-        if k == NB - 1:
-            break
-        mag = pr * pr + pi * pi
-        inv_r = pr / mag
-        inv_i = -pi / mag
         below = row_id > k
-        fr = jnp.where(below, col_r * inv_r - col_i * inv_i, 0.0)
-        fi = jnp.where(below, col_r * inv_i + col_i * inv_r, 0.0)
-        row_r = wr[k : k + 1]
-        row_i = wi[k : k + 1]
-        wr, wi = (
-            wr - (fr * row_r - fi * row_i),
-            wi - (fr * row_i + fi * row_r),
-        )
-    pr = jnp.concatenate(pivots_r, axis=0)
-    pi = jnp.concatenate(pivots_i, axis=0)
+        for n, (wr, wi) in enumerate(tiles):
+            col_r = jnp.take_along_axis(wr, where, axis=1)
+            col_i = jnp.take_along_axis(wi, where, axis=1)
+            pr = col_r[k : k + 1]
+            pi = col_i[k : k + 1]
+            pivots[n][0].append(pr)
+            pivots[n][1].append(pi)
+            if k == NB - 1:
+                continue
+            mag = pr * pr + pi * pi
+            inv_r = pr / mag
+            inv_i = -pi / mag
+            fr = jnp.where(below, col_r * inv_r - col_i * inv_i, 0.0)
+            fi = jnp.where(below, col_r * inv_i + col_i * inv_r, 0.0)
+            row_r = wr[k : k + 1]
+            row_i = wi[k : k + 1]
+            tiles[n] = (
+                wr - (fr * row_r - fi * row_i),
+                wi - (fr * row_i + fi * row_r),
+            )
+    return [unit_product(*(jnp.concatenate(part, axis=0) for part in p)) for p in pivots]
+
+
+def unit_product(pr, pi):
     mag = jnp.sqrt(pr * pr + pi * pi)
     ur = pr / mag
     ui = pi / mag
@@ -85,9 +89,8 @@
 def kernel(
     bands, umk, coeffs, flux, links,
     cv, perm, u, zm, zp, xp, xm, szm, szp, sxp, sxm, wb, xb,
-    acc_a, acc_b, acc_d, left_src, left_dst, down_src, down_dst,
-    unit, unit_x, unit_y,
-    hop, load_sem, send_sem, recv_sem, ez_sem, part_sem, unit_sem, hop_sem,
+    acc_a, acc_b, acc_d, left_src, left_dst, down_src, down_dst, corner_src, corner_dst,
+    hop, load_sem, send_sem, recv_sem, ez_sem, part_sem, hop_sem,
 ):
     i = lax.axis_index("kx")
     j = lax.axis_index("ky")
@@ -136,9 +139,9 @@
     gets_from = (None, None, shifted(4, 0), shifted(-4, 0))
 
     barrier = pltpu.get_barrier_semaphore()
-    for device in (right, left, up, down):
+    for device in (right, left, up, down, shifted(1, 1), shifted(-1, -1)):
         pl.semaphore_signal(barrier, inc=1, device_id=device, device_id_type=MESH)
-    arrivals = jnp.int32(4)
+    arrivals = jnp.int32(6)
     for flags, devices in (
         (sends_by, relay_of),
         (is_relay, relay_from),
@@ -384,66 +387,59 @@
     d_high = complex_parts(acc_d[...])
     none = jnp.zeros((NB, NB), F32)
 
+    lane = lax.broadcasted_iota(jnp.int32, (NB, 128), 1)
+    low, high = [], []
     for part in range(2):
         rows = pl.ds(part * NB, NB)
-        left_src[rows, :] = jnp.concatenate([x_low[part], none, d_low[part], none], axis=1)
-        down_src[rows, :] = jnp.concatenate([none, y_high[part], d_high[part], none], axis=1)
+        low.append(jnp.concatenate([x_low[part], y_low[part], d_low[part], none], axis=1))
+        high.append(jnp.concatenate([x_high[part], y_high[part], d_high[part], none], axis=1))
+        left_src[rows, :] = low[part]
+        down_src[rows, :] = high[part]
+        corner_src[rows, :] = jnp.where(lane < NB, low[part], high[part])
 
     def part_copy(which):
-        src, dst, device = ((left_src, left_dst, left), (down_src, down_dst, down))[which]
+        src, dst, device = (
+            (left_src, left_dst, left),
+            (down_src, down_dst, down),
+            (corner_src, corner_dst, shifted(-1, -1)),
+        )[which]
         return pltpu.make_async_remote_copy(
             src_ref=src, dst_ref=dst, send_sem=part_sem.at[0, which],
             recv_sem=part_sem.at[1, which], device_id=device, device_id_type=MESH,
         )
 
-    for which in range(2):
+    for which in (2, 1, 0):
         part_copy(which).start()
-    own = [
-        jnp.concatenate([x_high[part], y_low[part], none, none], axis=1) for part in range(2)
-    ]
-    for which in range(2):
+    for which in range(3):
         part_copy(which).wait_recv()
-    wr, wi = (
-        own[part] + left_dst[pl.ds(part * NB, NB), :] + down_dst[pl.ds(part * NB, NB), :]
-        for part in range(2)
-    )
-    lane = lax.broadcasted_iota(jnp.int32, (NB, 128), 1)
-    unused = lane >= 3 * NB
-    wr = jnp.where(unused, 1.0, wr)
-    ur, ui = eliminate(wr, wi)
-    unit[0:1, :] = ur
-    unit[1:2, :] = ui
-
-    def unit_copy(which):
-        dst, device = ((unit_x, left), (unit_y, down))[which]
-        return pltpu.make_async_remote_copy(
-            src_ref=unit, dst_ref=dst, send_sem=unit_sem.at[0, which],
-            recv_sem=unit_sem.at[1, which], device_id=device, device_id_type=MESH,
-        )
-
-    for which in range(2):
-        unit_copy(which).start()
-    for which in range(2):
-        unit_copy(which).wait_recv()
+    own_tile, next_tile = [], []
+    for part in range(2):
+        rows = pl.ds(part * NB, NB)
+        of_left, of_down, of_corner = left_dst[rows, :], down_dst[rows, :], corner_dst[rows, :]
+        other = jnp.where(lane < 2 * NB, low[part] + of_down, of_left + of_down)
+        other = jnp.where(lane < NB, high[part] + of_left, other)
+        own_tile.append(jnp.where(lane < 3 * NB, other, 1.0))
+        other = of_corner + jnp.where(lane < NB, of_down, of_left)
+        next_tile.append(jnp.where(lane < 2 * NB, other, 1.0))
+    unit, unit_next = eliminate((own_tile, next_tile))
 
     def group(ref, which):
-        real, imag = ref[0:1, :], ref[1:2, :]
+        real, imag = ref
         if which:
             shift = 128 - which * NB
             real, imag = pltpu.roll(real, shift, 1), pltpu.roll(imag, shift, 1)
         return real, imag
 
     along_x, along_y, along_d = (group(unit, which) for which in range(3))
-    y_next = group(unit_x, 1)
-    x_next = group(unit_y, 0)
+    y_next = group(unit_next, 1)
+    x_next = group(unit_next, 0)
     first = times(times(along_x, y_next), conjugate(along_d))
     second = times(times(along_d, conjugate(x_next)), conjugate(along_y))
-    is_real = lax.broadcasted_iota(jnp.int32, (1, 128), 1) == 0
+    lane = lax.broadcasted_iota(jnp.int32, (1, 128), 1)
     angle = jnp.arctan2(
-        jnp.where(is_real, first[1], second[1]), jnp.where(is_real, first[0], second[0])
+        jnp.where(lane == 0, first[1], second[1]), jnp.where(lane == 0, first[0], second[0])
     )
     flux[0] = angle[:, :2]
-    lane = lax.broadcasted_iota(jnp.int32, (1, 128), 1)
     for part in range(2):
         row = jnp.where(lane == 0, along_x[part], along_y[part])
         row = jnp.where(lane == 2, along_d[part], row)
@@ -469,9 +465,8 @@
             for c in RELAYED[stream]:
                 relay_copy(stream, c).wait_send()
 
-    for which in range(2):
+    for which in range(3):
         part_copy(which).wait_send()
-        unit_copy(which).wait_send()
 
 
 def per_device(coeffs, bands, umklapp):
@@ -503,16 +498,14 @@
             pltpu.VMEM((ROWS, 128), F32),
             pltpu.VMEM((ROWS, 128), F32),
             pltpu.VMEM((ROWS, 128), F32),
-            pltpu.VMEM((8, 128), F32),
-            pltpu.VMEM((8, 128), F32),
-            pltpu.VMEM((8, 128), F32),
+            pltpu.VMEM((ROWS, 128), F32),
+            pltpu.VMEM((ROWS, 128), F32),
             pltpu.VMEM((max(map(len, RELAYED)) * CHUNK, ROWS, GY), bf16),
             pltpu.SemaphoreType.DMA((GX // TILE,)),
             pltpu.SemaphoreType.DMA((4, NCHUNK)),
             pltpu.SemaphoreType.DMA((4, NCHUNK)),
             pltpu.SemaphoreType.DMA((2, 2)),
-            pltpu.SemaphoreType.DMA((2, 2)),
-            pltpu.SemaphoreType.DMA((2, 2)),
+            pltpu.SemaphoreType.DMA((2, 3)),
             pltpu.SemaphoreType.DMA((2, NCHUNK)),
         ],
         compiler_params=pltpu.CompilerParams(

time: 78.1 us -> 77.6 us (level)
  no operation moved by 1% of the time
where the time goes in v5:
time: 77.6 us; the launch traced here: 77.5 us
  Pallas kernels  74.5 us (96%)
  local copies, waits for them, and re-layouts  2.36 us (3%)
    pallas_call x1, Pallas kernels, per_device(): pl.pallas_call(kernel, out_shape=(jax.ShapeDtypeStruct((1, 1, 2), F32), j...  74.5 us
    unnamed x2, local copies, waits for them, and re-layouts  2.36 us

profile of v5, /device:TPU:1, one launch (start us, length us, event | category | flops | bytes accessed | tf_op | source)
XLA Modules:
  0.0 77.5 jit_solution(9629145555121502066)
XLA Ops:
  0.6 74.5 %shard_map.50 = (f32[1,1,2]{2,1,0:T(1,128)}, f32[1,1,2,3]{3,2,1,0:T(2,128)}) custom-call(s32[32]{0:T(128)} %bands.1, s32[2,2]{1,0:T(2,128)} %umk.1, bf16[2,36,128,256]{3,2,1,0:T(8,128)(2,1)} %bitcast.2), custom_call_target="tpu_custom_call" | custom-call | tf_op jit(solution)/shard_map/pallas_call | solution.py:476
  75.1 1.1 %copy.7 = f32[1,1,2]{2,1,0:T(1,128)} copy(f32[1,1,2]{2,1,0:T(1,128)} %get-tuple-element.8) | data formatting | bytes 16
  76.2 1.2 %copy.8 = f32[1,1,3,2]{2,3,1,0:T(2,128)} copy(f32[1,1,3,2]{2,3,1,0:T(2,128)} %bitcast.3) | data formatting | bytes 48

commit v6 on v5

--- a/solution.py
+++ b/solution.py
@@ -20,6 +20,7 @@
 GROUP = 8
 RELAYED = ((1,), (1,), (4, 5, 6, 7), (4, 5, 6, 7))
 LATE = 4
+PANEL = 4
 F32 = jnp.float32
 CONTRACT = (((1,), (1,)), ((), ()))
 
@@ -34,7 +35,7 @@
     return real, imag
 
 
-def times(a, b):
+def product(a, b):
     return a[0] * b[0] - a[1] * b[1], a[0] * b[1] + a[1] * b[0]
 
 
@@ -42,35 +43,43 @@
     return a[0], -a[1]
 
 
+def less(a, b):
+    return a[0] - b[0], a[1] - b[1]
+
+
 def eliminate(tiles):
-    lane = lax.broadcasted_iota(jnp.int32, (NB, 128), 1)
-    row_id = lax.broadcasted_iota(jnp.int32, (NB, 128), 0)
-    base = (lane // NB) * NB
-    tiles = list(tiles)
+    tiles = [tuple(tile) for tile in tiles]
     pivots = [([], []) for _ in tiles]
-    for k in range(NB):
-        where = base + k
-        below = row_id > k
-        for n, (wr, wi) in enumerate(tiles):
-            col_r = jnp.take_along_axis(wr, where, axis=1)
-            col_i = jnp.take_along_axis(wi, where, axis=1)
-            pr = col_r[k : k + 1]
-            pi = col_i[k : k + 1]
-            pivots[n][0].append(pr)
-            pivots[n][1].append(pi)
-            if k == NB - 1:
-                continue
-            mag = pr * pr + pi * pi
-            inv_r = pr / mag
-            inv_i = -pi / mag
-            fr = jnp.where(below, col_r * inv_r - col_i * inv_i, 0.0)
-            fi = jnp.where(below, col_r * inv_i + col_i * inv_r, 0.0)
-            row_r = wr[k : k + 1]
-            row_i = wi[k : k + 1]
-            tiles[n] = (
-                wr - (fr * row_r - fi * row_i),
-                wi - (fr * row_i + fi * row_r),
-            )
+    for start in range(0, NB, PANEL):
+        count = tiles[0][0].shape[0]
+        offset = start - (NB - count)
+        lane = lax.broadcasted_iota(jnp.int32, (count, 128), 1)
+        row_id = lax.broadcasted_iota(jnp.int32, (count, 128), 0)
+        base = (lane // NB) * NB + start
+        for n, work in enumerate(tiles):
+            cols = [
+                tuple(jnp.take_along_axis(w, base + e, axis=1) for w in work)
+                for e in range(PANEL)
+            ]
+            rows = [tuple(w[offset + e : offset + e + 1] for w in work) for e in range(PANEL)]
+            for e in range(PANEL):
+                at = offset + e
+                pivot = tuple(c[at : at + 1] for c in cols[e])
+                for part in range(2):
+                    pivots[n][part].append(pivot[part])
+                if start + e == NB - 1:
+                    break
+                scale = 1.0 / (pivot[0] * pivot[0] + pivot[1] * pivot[1])
+                factor = product(cols[e], (pivot[0] * scale, -pivot[1] * scale))
+                factor = tuple(jnp.where(row_id > at, f, 0.0) for f in factor)
+                for g in range(e + 1, PANEL):
+                    cols[g] = less(cols[g], product(factor, [c[at : at + 1] for c in cols[g]]))
+                    piece = [f[offset + g : offset + g + 1] for f in factor]
+                    rows[g] = less(rows[g], product(piece, rows[e]))
+                if start + PANEL < NB:
+                    work = less(work, product(factor, rows[e]))
+            drop = (offset + PANEL) // 8 * 8
+            tiles[n] = tuple(w[drop:] for w in work)
     return [unit_product(*(jnp.concatenate(part, axis=0) for part in p)) for p in pivots]
 
 
@@ -87,10 +96,11 @@
 
 
 def kernel(
-    bands, umk, coeffs, flux, links,
+    bands_in, umk_in, coeffs, flux, links,
     cv, perm, u, zm, zp, xp, xm, szm, szp, sxp, sxm, wb, xb,
     acc_a, acc_b, acc_d, left_src, left_dst, down_src, down_dst, corner_src, corner_dst,
     hop, load_sem, send_sem, recv_sem, ez_sem, part_sem, hop_sem,
+    bands, umk, index_sem,
 ):
     i = lax.axis_index("kx")
     j = lax.axis_index("ky")
@@ -109,6 +119,12 @@
         return pltpu.make_async_copy(coeffs.at[:, :, rows, :], cv[t], load_sem.at[t])
 
     half_tiles = HALF // TILE
+    indices = [
+        pltpu.make_async_copy(bands_in, bands, index_sem.at[0]),
+        pltpu.make_async_copy(umk_in, umk, index_sem.at[1]),
+    ]
+    for copy in indices:
+        copy.start()
     load(0).start()
     load(half_tiles).start()
 
@@ -157,6 +173,8 @@
             def _(device=device):
                 pl.semaphore_signal(barrier, inc=1, device_id=device, device_id_type=MESH)
 
+    for copy in indices:
+        copy.wait()
     zero = jnp.int32(0)
     ax = jnp.where(x_edge, umk[0, 0], zero)
     bx = jnp.where(x_edge, umk[0, 1], zero)
@@ -330,8 +348,10 @@
     @pl.loop(0, NCHUNK)
     def _(step):
         early, late = RELAYED[0][0], len(RELAYED[0])
+        turn = NCHUNK - 1 - late
         c = jnp.where(step < early, step, step + late)
-        c = jnp.where(step < NCHUNK - late, c, early + step - (NCHUNK - late))
+        c = jnp.where(step < turn, c, early + step - turn)
+        c = jnp.where(step == NCHUNK - 1, step, c)
         for stream in range(4):
             stream_wait(stream, c).wait_recv()
         first = c * CHUNK
@@ -433,8 +453,8 @@
     along_x, along_y, along_d = (group(unit, which) for which in range(3))
     y_next = group(unit_next, 1)
     x_next = group(unit_next, 0)
-    first = times(times(along_x, y_next), conjugate(along_d))
-    second = times(times(along_d, conjugate(x_next)), conjugate(along_y))
+    first = product(product(along_x, y_next), conjugate(along_d))
+    second = product(product(along_d, conjugate(x_next)), conjugate(along_y))
     lane = lax.broadcasted_iota(jnp.int32, (1, 128), 1)
     angle = jnp.arctan2(
         jnp.where(lane == 0, first[1], second[1]), jnp.where(lane == 0, first[0], second[0])
@@ -480,9 +500,9 @@
             jax.ShapeDtypeStruct((1, 1, 2, 3), F32),
         ),
         in_specs=[
-            pl.BlockSpec(memory_space=pltpu.SMEM),
-            pl.BlockSpec(memory_space=pltpu.SMEM),
-            pl.BlockSpec(memory_space=pl.ANY),
+            pl.BlockSpec(memory_space=pltpu.HBM),
+            pl.BlockSpec(memory_space=pltpu.HBM),
+            pl.BlockSpec(memory_space=pltpu.HBM),
         ],
         out_specs=(pl.BlockSpec(memory_space=pltpu.VMEM),) * 2,
         scratch_shapes=[
@@ -507,11 +527,14 @@
             pltpu.SemaphoreType.DMA((2, 2)),
             pltpu.SemaphoreType.DMA((2, 3)),
             pltpu.SemaphoreType.DMA((2, NCHUNK)),
+            pltpu.SMEM((NB,), jnp.int32),
+            pltpu.SMEM((2, 2), jnp.int32),
+            pltpu.SemaphoreType.DMA((2,)),
         ],
         compiler_params=pltpu.CompilerParams(
-            collective_id=0, has_side_effects=True, vmem_limit_bytes=56 << 20
+            collective_id=0, has_side_effects=True, vmem_limit_bytes=50 << 20
         ),
-    )(bands, umklapp, coeffs[0, 0])
+    )(*(pltpu.with_memory_space_constraint(v, pltpu.HBM) for v in (bands, umklapp, coeffs[0, 0])))
     return flux, jnp.swapaxes(links, 2, 3)
 
 

time: 77.6 us -> 73.1 us (0.942)
  Pallas kernels: 74.5 us -> 71.3 us
  local copies, waits for them, and re-layouts: 2.36 us -> 1.07 us
    pallas_call x1, Pallas kernels: 74.5 us -> 71.3 us  [per_device(): pl.pallas_call(kernel, out_shape=(jax.ShapeDtypeStruct((1, 1, 2), F32), j...]
    unnamed x2, local copies, waits for them, and re-layouts: 2.36 us -> 1.07 us
where the time goes in v6:
time: 73.1 us; the launch traced here: 73 us
  Pallas kernels  71.3 us (98%)
  local copies, waits for them, and re-layouts  1.07 us (1%)
    pallas_call x1, Pallas kernels, per_device(): pl.pallas_call(kernel, out_shape=(jax.ShapeDtypeStruct((1, 1, 2), F32), j...  71.3 us

profile of v6, /device:TPU:1, one launch (start us, length us, event | category | flops | bytes accessed | tf_op | source)
XLA Modules:
  0.0 73.0 jit_solution(1357797018920989074)
XLA Ops:
  0.6 71.3 %shard_map.50 = (f32[1,1,2]{2,1,0:T(1,128)S(1)}, f32[1,1,2,3]{3,2,1,0:T(2,128)S(1)}) custom-call(s32[32]{0:T(128)} %bands_in.1, s32[2,2]{1,0:T(2,128)} %umk_in.1, bf16[2,36,128,256]{3,2,1,0:T(8,128)(2,1)} %bitcast.3), custom_call_target="tpu_custom_call" | custom-call | tf_op jit(solution)/shard_map/pallas_call | solution.py:496
  71.9 0.5 copy.7
  72.4 0.6 copy.8

commit v7 on v6

--- a/solution.py
+++ b/solution.py
@@ -345,77 +345,78 @@
     build(wb, HALF, HALF, -ay, bx - by)
     build(xb, HALF, HALF, ax, bx - by)
 
-    @pl.loop(0, NCHUNK)
+    def diagonal(place, row, count):
+        total = None
+        for q in range(count):
+            source = row + q - ax
+            inside = jnp.logical_and(source >= 0, source < HALF)
+            target = jnp.where(inside, source - ay, 0)
+            target = jnp.where(target < 0, target + HALF + EXTRA, target)
+            left_rows = zp[place + q]
+            term = dot(jnp.where(inside, left_rows, jnp.zeros_like(left_rows)), xm[target])
+            total = term if total is None else total + term
+        acc_d[...] += total
+
+    @pl.when(edge)
+    def _():
+        for c in range(NCHUNK):
+            stream_wait(3, c).wait_recv()
+
+    @pl.when(y_edge)
+    def _():
+        extra(1, sxm, xm, left).wait_recv()
+
+    @pl.when(x_edge)
+    def _():
+        extra(0, szp, zp, up).wait_recv()
+        diagonal(HALF, jnp.where(ax > 0, HALF, -EXTRA), EXTRA)
+
+    def low_terms(c):
+        stream_wait(0, c).wait_recv()
+        stream_wait(2, c).wait_recv()
+        total = None
+        for q in range(CHUNK):
+            p = c * CHUNK + q
+            own = u[p]
+            term = dot(
+                jnp.concatenate([own, xp[p]], axis=0), jnp.concatenate([zm[p], own], axis=0)
+            )
+            total = term if total is None else total + term
+        acc_a[...] += total
+
+    def high_terms(c):
+        stream_wait(1, c).wait_recv()
+
+        @pl.when(jnp.logical_not(edge))
+        def _():
+            stream_wait(3, c).wait_recv()
+
+        total = None
+        for q in range(CHUNK):
+            p = c * CHUNK + q
+            term = dot(
+                jnp.concatenate([zp[p], xb[p]], axis=0), jnp.concatenate([wb[p], xm[p]], axis=0)
+            )
+            total = term if total is None else total + term
+        acc_b[...] += total
+
+        @pl.when(edge)
+        def _():
+            diagonal(c * CHUNK, c * CHUNK, CHUNK)
+
+    @pl.loop(0, NCHUNK - 1)
     def _(step):
         early, late = RELAYED[0][0], len(RELAYED[0])
         turn = NCHUNK - 1 - late
         c = jnp.where(step < early, step, step + late)
         c = jnp.where(step < turn, c, early + step - turn)
-        c = jnp.where(step == NCHUNK - 1, step, c)
-        for stream in range(4):
-            stream_wait(stream, c).wait_recv()
-        first = c * CHUNK
-        a = None
-        b = None
-        for q in range(CHUNK):
-            p = first + q
-            own = u[p]
-            lhs = jnp.concatenate([own, xp[p]], axis=0)
-            rhs = jnp.concatenate([zm[p], own], axis=0)
-            term = dot(lhs, rhs)
-            a = term if a is None else a + term
-            lhs = jnp.concatenate([zp[p], xb[p]], axis=0)
-            rhs = jnp.concatenate([wb[p], xm[p]], axis=0)
-            term = dot(lhs, rhs)
-            b = term if b is None else b + term
-        acc_a[...] += a
-        acc_b[...] += b
-
-    acc_d[...] = acc_b[:ROWS, ROWS:]
-
-    @pl.when(x_edge)
-    def _():
-        extra(0, szp, zp, up).wait_recv()
-
-    @pl.when(y_edge)
-    def _():
-        extra(1, sxm, xm, left).wait_recv()
-
-    @pl.when(edge)
-    def _():
-        acc_d[...] = jnp.zeros_like(acc_d)
-
-        @pl.loop(0, HALF // 32)
-        def _(c):
-            total = None
-            for q in range(32):
-                s = c * 32 + q + ax
-                t = c * 32 + q - ay
-                s = jnp.where(s < 0, s + HALF + EXTRA, s)
-                t = jnp.where(t < 0, t + HALF + EXTRA, t)
-                term = dot(zp[s], xm[t])
-                total = term if total is None else total + term
-            acc_d[...] += total
-
-    a = acc_a[...]
-    b = acc_b[...]
-    d_low = complex_parts(a[ROWS:, :ROWS])
-    x_low = complex_parts(a[ROWS:, ROWS:])
-    y_low = complex_parts(a[:ROWS, :ROWS])
-    y_high = complex_parts(b[:ROWS, :ROWS])
-    x_high = complex_parts(b[ROWS:, ROWS:])
-    d_high = complex_parts(acc_d[...])
+        low_terms(c)
+        high_terms(c)
+
     none = jnp.zeros((NB, NB), F32)
 
-    lane = lax.broadcasted_iota(jnp.int32, (NB, 128), 1)
-    low, high = [], []
-    for part in range(2):
-        rows = pl.ds(part * NB, NB)
-        low.append(jnp.concatenate([x_low[part], y_low[part], d_low[part], none], axis=1))
-        high.append(jnp.concatenate([x_high[part], y_high[part], d_high[part], none], axis=1))
-        left_src[rows, :] = low[part]
-        down_src[rows, :] = high[part]
-        corner_src[rows, :] = jnp.where(lane < NB, low[part], high[part])
+    def table(x, y, d):
+        return [jnp.concatenate([x[part], y[part], d[part], none], axis=1) for part in range(2)]
 
     def part_copy(which):
         src, dst, device = (
@@ -428,15 +429,43 @@
             recv_sem=part_sem.at[1, which], device_id=device, device_id_type=MESH,
         )
 
-    for which in (2, 1, 0):
-        part_copy(which).start()
+    low_terms(NCHUNK - 1)
+    a = acc_a[...]
+    low = table(
+        complex_parts(a[ROWS:, ROWS:]),
+        complex_parts(a[:ROWS, :ROWS]),
+        complex_parts(a[ROWS:, :ROWS]),
+    )
+    for part in range(2):
+        left_src[pl.ds(part * NB, NB), :] = low[part]
+    part_copy(0).start()
+
+    high_terms(NCHUNK - 1)
+
+    @pl.when(jnp.logical_not(edge))
+    def _():
+        acc_d[...] = acc_b[:ROWS, ROWS:]
+
+    b = acc_b[...]
+    high = table(
+        complex_parts(b[ROWS:, ROWS:]),
+        complex_parts(b[:ROWS, :ROWS]),
+        complex_parts(acc_d[...]),
+    )
+    lane = lax.broadcasted_iota(jnp.int32, (NB, 128), 1)
+    for part in range(2):
+        rows = pl.ds(part * NB, NB)
+        down_src[rows, :] = high[part]
+        corner_src[rows, :] = jnp.where(lane < NB, left_src[rows, :], high[part])
+    part_copy(1).start()
+    part_copy(2).start()
     for which in range(3):
         part_copy(which).wait_recv()
     own_tile, next_tile = [], []
     for part in range(2):
         rows = pl.ds(part * NB, NB)
         of_left, of_down, of_corner = left_dst[rows, :], down_dst[rows, :], corner_dst[rows, :]
-        other = jnp.where(lane < 2 * NB, low[part] + of_down, of_left + of_down)
+        other = jnp.where(lane < 2 * NB, left_src[rows, :] + of_down, of_left + of_down)
         other = jnp.where(lane < NB, high[part] + of_left, other)
         own_tile.append(jnp.where(lane < 3 * NB, other, 1.0))
         other = of_corner + jnp.where(lane < NB, of_down, of_left)

time: 73.1 us -> 71.1 us (0.973)
  Pallas kernels: 71.3 us -> 69.3 us
    pallas_call x1, Pallas kernels: 71.3 us -> 69.3 us  [per_device(): pl.pallas_call(kernel, out_shape=(jax.ShapeDtypeStruct((1, 1, 2), F32), j...]
where the time goes in v7:
time: 71.1 us; the launch traced here: 71 us
  Pallas kernels  69.3 us (97%)
  local copies, waits for them, and re-layouts  1.07 us (2%)
    pallas_call x1, Pallas kernels, per_device(): pl.pallas_call(kernel, out_shape=(jax.ShapeDtypeStruct((1, 1, 2), F32), j...  69.3 us

profile of v7, /device:TPU:1, one launch (start us, length us, event | category | flops | bytes accessed | tf_op | source)
XLA Modules:
  0.0 71.0 jit_solution(4374952975070966265)
XLA Ops:
  0.6 69.3 %shard_map.50 = (f32[1,1,2]{2,1,0:T(1,128)S(1)}, f32[1,1,2,3]{3,2,1,0:T(2,128)S(1)}) custom-call(s32[32]{0:T(128)} %bands_in.1, s32[2,2]{1,0:T(2,128)} %umk_in.1, bf16[2,36,128,256]{3,2,1,0:T(8,128)(2,1)} %bitcast.3), custom_call_target="tpu_custom_call" | custom-call | tf_op jit(solution)/shard_map/pallas_call | solution.py:525
  69.9 0.5 copy.7
  70.4 0.6 copy.8

commit v8 on v7

--- a/solution.py
+++ b/solution.py
@@ -19,7 +19,7 @@
 TILE = 16
 GROUP = 8
 RELAYED = ((1,), (1,), (4, 5, 6, 7), (4, 5, 6, 7))
-LATE = 4
+LATE = 5
 PANEL = 4
 F32 = jnp.float32
 CONTRACT = (((1,), (1,)), ((), ()))
@@ -125,8 +125,8 @@
     ]
     for copy in indices:
         copy.start()
+    load(half_tiles).start()
     load(0).start()
-    load(half_tiles).start()
 
     def shifted(di, dj):
         return lax.rem(i + di + ni, ni), lax.rem(j + dj + nj, nj)
@@ -271,15 +271,14 @@
             u[rows, pl.ds(g * TILE, TILE), :] = moved
 
     for t in range(half_tiles):
-        load(t).wait()
-        gather(t)
-        load(t + half_tiles).wait()
-        gather(t + half_tiles)
-        if t == 0:
-            pl.semaphore_wait(barrier, arrivals)
-        for c in range(t * TILE // CHUNK, (t + 1) * TILE // CHUNK):
-            for stream in range(4):
-                stream_send(stream, c, False, jnp.logical_not(need[stream]), True)
+        for tile, streams in ((t + half_tiles, (1, 3)), (t, (0, 2))):
+            load(tile).wait()
+            gather(tile)
+            if tile == half_tiles:
+                pl.semaphore_wait(barrier, arrivals)
+            for c in range(t * TILE // CHUNK, (t + 1) * TILE // CHUNK):
+                for stream in streams:
+                    stream_send(stream, c, False, jnp.logical_not(need[stream]), True)
 
     def build(dst, count, first, dp, dq):
         shift = lax.rem(GY - dq, GY)

time: 71.1 us -> 71.1 us (level)
  no operation moved by 1% of the time
where the time goes in v8:
time: 71.1 us; the launch traced here: 71 us
  Pallas kernels  69.3 us (97%)
  local copies, waits for them, and re-layouts  1.07 us (2%)
    pallas_call x1, Pallas kernels, per_device(): pl.pallas_call(kernel, out_shape=(jax.ShapeDtypeStruct((1, 1, 2), F32), j...  69.3 us

profile of v8, /device:TPU:1, one launch (start us, length us, event | category | flops | bytes accessed | tf_op | source)
XLA Modules:
  0.0 71.0 jit_solution(13157857698375476908)
XLA Ops:
  0.6 69.3 %shard_map.50 = (f32[1,1,2]{2,1,0:T(1,128)S(1)}, f32[1,1,2,3]{3,2,1,0:T(2,128)S(1)}) custom-call(s32[32]{0:T(128)} %bands_in.1, s32[2,2]{1,0:T(2,128)} %umk_in.1, bf16[2,36,128,256]{3,2,1,0:T(8,128)(2,1)} %bitcast.3), custom_call_target="tpu_custom_call" | custom-call | tf_op jit(solution)/shard_map/pallas_call | solution.py:524
  69.9 0.5 copy.7
  70.4 0.6 copy.8
